TPU v7x, 32 devices: a whole 2x2x4 slice. The times are simulated.
32 devices in a mesh: facet: 4 (over y, x), col: 8 (over z, core).
Axes of the slice: x: 2, y: 2, z: 4, core: 2. Of those that a mesh axis runs over, the one named last changes fastest.
Arguments:
- facets: bfloat16 [4, 2, 768, 768], P('facet', None, 'col'), may hold values from -6 to 6
- col_offsets: int32 [8], replicated, may hold values from 0 to 767
- sub_rows: int32 [4, 8], P(None, 'col'), may hold values from 0 to 767
- facet_offsets: int32 [4, 2], replicated, may hold values from 0 to 320
- vis_pos: int32 [4, 8, 2, 256], P('facet', 'col'), may hold values from 0 to 1535
- observed: float32 [4, 8, 2, 256], P('facet', 'col'), may hold values from -6 to 6
Outputs:
- predicted: float32 [4, 8, 2, 256], P('facet', 'col')
- facet_update: float32 [4, 2, 768, 768], P('facet', None, 'col')
All inputs are finite; a program needn't handle non-finite values.
Results may differ from a plain program's by a relative error of at most 0.0085.
Values may be sent and summed in bfloat16 or wider, within the bound.
A program may use at most 64 MiB of HBM per device.

v0:
```python
import functools
import math

import jax
import jax.numpy as jnp
from jax import lax
from jax.experimental import pallas as pl
from jax.experimental.pallas import tpu as pltpu
from jax.sharding import PartitionSpec as P

M = 64
SUB = 384
FINE = 1536
YN = 768
MESH = pl.DeviceIdType.MESH
F32 = jnp.float32
BF16 = jnp.bfloat16


def cis(product, modulus, direction):
    turns = jnp.floor(product * (1.0 / modulus) + 0.5)
    half = (product - turns * modulus) * (direction * math.pi / modulus)
    z = half * half
    s = half * (1.0 + z * (-1 / 6 + z * (1 / 120 + z * (-1 / 5040 + z * (1 / 362880 + z * (-1 / 39916800))))))
    c = 1.0 + z * (-1 / 2 + z * (1 / 24 + z * (-1 / 720 + z * (1 / 40320 + z * (-1 / 3628800 + z * (1 / 479001600))))))
    return 1.0 - 2.0 * s * s, 2.0 * s * c


def iota(shape, axis):
    return lax.broadcasted_iota(jnp.int32, shape, axis).astype(F32)


def dot(left, right, dims):
    return lax.dot_general(left, right, (dims, ((), ())), preferred_element_type=F32)


NN = ((1,), (0,))
NT = ((1,), (1,))
TN = ((0,), (0,))


def kernel(
    n_facet,
    n_col,
    facets_hbm,
    col_offsets,
    sub_rows,
    facet_offsets,
    vis_pos,
    observed,
    predicted,
    update,
    facet_buf,
    base,
    turn,
    wall,
    subt,
    subt_t,
    u_tab,
    v_tab,
    strip_out,
    strip_in,
    contrib_out,
    contrib_in,
    back_out,
    back_in,
    delta_out,
    delta_in,
    load_sem,
    col_send,
    col_recv,
    facet_send,
    facet_recv,
):
    my_f = lax.axis_index("facet")
    my_c = lax.axis_index("col")
    n_rows = facet_buf.shape[1]
    n_vis = vis_pos.shape[3]

    load = pltpu.make_async_copy(facets_hbm.at[0], facet_buf, load_sem)
    load.start()
    barrier = pltpu.get_barrier_semaphore()
    col_order = [lax.rem(my_c + n_col // 2 + i, n_col) for i in range(n_col)]
    col_order = [c for i, c in enumerate(col_order) if i != n_col // 2] + [my_c]
    facet_order = [lax.rem(my_f + 1 + i, n_facet) for i in range(n_facet)]
    for c in col_order[:-1]:
        pl.semaphore_signal(barrier, inc=1, device_id=(my_f, c), device_id_type=MESH)
    for f in facet_order[:-1]:
        pl.semaphore_signal(barrier, inc=1, device_id=(f, my_c), device_id_type=MESH)

    def col_copy(phase, out, into, slot_out, slot_in, target):
        return pltpu.make_async_remote_copy(
            src_ref=out.at[slot_out],
            dst_ref=into.at[slot_in],
            send_sem=col_send.at[phase, slot_out],
            recv_sem=col_recv.at[phase, slot_in],
            device_id=(my_f, target),
            device_id_type=MESH,
        )

    def facet_copy(phase, out, into, slot_out, slot_in, target):
        return pltpu.make_async_remote_copy(
            src_ref=out.at[slot_out],
            dst_ref=into.at[slot_in],
            send_sem=facet_send.at[phase, slot_out],
            recv_sem=facet_recv.at[phase, slot_in],
            device_id=(target, my_c),
            device_id_type=MESH,
        )

    base_re, base_im = cis(iota((M, YN), 0) * iota((M, YN), 1), YN, -1.0)
    inv_root = 1.0 / math.sqrt(YN)
    base[0] = base_re * inv_root
    base[1] = base_im * inv_root
    along = iota((1, YN), 1)
    for c in range(n_col):
        turn[0, pl.ds(c, 1)] = along * col_offsets[c].astype(F32)
    for s in range(n_facet):
        turn[0, pl.ds(n_col + s, 1)] = along * sub_rows[s, 0].astype(F32)
    turn_re, turn_im = cis(turn[0], YN, -1.0)
    turn[0] = turn_re
    turn[1] = turn_im

    def table(into, row, slot):
        re, im = turn[0, pl.ds(row, 1)], turn[1, pl.ds(row, 1)]
        into[slot, :M] = (base[0] * re - base[1] * im).astype(BF16)
        into[slot, M:] = (base[0] * im + base[1] * re).astype(BF16)

    lane = lax.broadcasted_iota(jnp.int32, (1, 2 * M), 1)
    minus_plus = jnp.where(lane < M, -1.0, 1.0)

    def swapped(value):
        return pltpu.roll(value, M, 1)

    load.wait()
    both = facet_buf[...]
    if n_rows % 16:
        both = both.astype(F32).reshape(2 * n_rows, YN).astype(BF16)
    else:
        both = both.reshape(2 * n_rows, YN)
    for i, c in enumerate(col_order):
        table(wall, c, c)
        prod = dot(both, wall[c], NT)
        part = (prod[:n_rows] + minus_plus * swapped(prod[n_rows:])).astype(BF16)
        if i == 0:
            pl.semaphore_wait(barrier, n_col - 1 + n_facet - 1)
        if i < n_col - 1:
            strip_out[c] = part
            col_copy(0, strip_out, strip_in, c, my_c, c).start()
        else:
            strip_in[c] = part

    for s in range(n_facet):
        table(subt, n_col + s, s)
    for tab, which in ((u_tab, 0), (v_tab, 1)):
        point = vis_pos[0, 0, pl.ds(which, 1)].astype(F32)
        low_re, low_im = cis(iota((M, n_vis), 0) * point, FINE, 1.0)
        low_re = low_re * (1.0 / math.sqrt(SUB))
        low_im = low_im * (1.0 / math.sqrt(SUB))
        for f in range(n_facet):
            high_re, high_im = cis(point * facet_offsets[f, which].astype(F32), FINE, 1.0)
            tab[f, :M] = (low_re * high_re - low_im * high_im).astype(tab.dtype)
            tab[f, M:] = (low_re * high_im + low_im * high_re).astype(tab.dtype)
    for s in range(n_facet):
        subt_t[:, 2 * M * s : 2 * M * (s + 1)] = subt[s].T

    for c in col_order[:-1]:
        col_copy(0, strip_out, strip_in, c, c, c).wait_recv()
    strip = strip_in[...]
    if n_rows % 16:
        strip = strip.astype(F32).reshape(YN, 2 * M).astype(BF16)
    else:
        strip = strip.reshape(YN, 2 * M)
    for i, s in enumerate(facet_order):
        prod = dot(subt[s], strip, NN)
        part = (prod[:M] + minus_plus * swapped(prod[M:])).astype(BF16)
        if i < n_facet - 1:
            contrib_out[s] = part
            facet_copy(0, contrib_out, contrib_in, s, my_f, s).start()
        else:
            contrib_in[s] = part

    pred_re = jnp.zeros((M, n_vis), F32)
    pred_im = jnp.zeros((M, n_vis), F32)
    for i in range(n_facet):
        f = facet_order[n_facet - 1 - i]
        if i > 0:
            facet_copy(0, contrib_out, contrib_in, f, f, f).wait_recv()
        with_re = dot(contrib_in[f], u_tab[f, :M], TN)
        with_im = dot(contrib_in[f], u_tab[f, M:], TN)
        rows_re = with_re[:M] - with_im[M:]
        rows_im = with_im[:M] + with_re[M:]
        v_re, v_im = v_tab[f, :M], v_tab[f, M:]
        pred_re += rows_re * v_re - rows_im * v_im
        pred_im += rows_re * v_im + rows_im * v_re
    pred_re = jnp.sum(pred_re, axis=0, keepdims=True)
    pred_im = jnp.sum(pred_im, axis=0, keepdims=True)
    predicted[0, 0, pl.ds(0, 1)] = pred_re
    predicted[0, 0, pl.ds(1, 1)] = pred_im
    weight = SUB / math.sqrt(n_vis)
    diff_re = pred_re - observed[0, 0, pl.ds(0, 1)]
    diff_im = pred_im - observed[0, 0, pl.ds(1, 1)]
    for i, f in enumerate(facet_order):
        v_re, v_im = v_tab[f, :M], v_tab[f, M:]
        wgt_re = ((diff_re * v_re + diff_im * v_im) * weight).astype(BF16)
        wgt_im = ((diff_im * v_re - diff_re * v_im) * weight).astype(BF16)
        prod = dot(u_tab[f], jnp.concatenate([wgt_re, wgt_im], axis=0), NT)
        part = (prod[:M] - minus_plus * swapped(prod[M:])).astype(BF16)
        if i < n_facet - 1:
            back_out[f] = part
            facet_copy(1, back_out, back_in, f, my_f, f).start()
        else:
            back_in[f] = part

    for s in facet_order[:-1]:
        facet_copy(1, back_out, back_in, s, s, s).wait_recv()
    stacked = []
    for s in range(n_facet):
        block = back_in[s]
        stacked += [block, (-minus_plus * swapped(block.astype(F32))).astype(BF16)]
    back_scale = math.sqrt(YN / (M * n_facet))
    delta = dot(subt_t[...], jnp.concatenate(stacked, axis=0), NN) * back_scale
    delta_out[...] = delta.reshape(n_col, n_rows, 2 * M).astype(BF16)
    for c in col_order[:-1]:
        col_copy(1, delta_out, delta_in, c, my_c, c).start()
    delta_in[my_c] = delta_out[my_c]

    for c in col_order[:-1]:
        col_copy(1, delta_out, delta_in, c, c, c).wait_recv()
    up_scale = math.sqrt(YN / (M * n_col))
    straight, crossed = [], []
    for c in range(n_col):
        block = delta_in[c]
        straight.append(block)
        crossed.append((-minus_plus * swapped(block.astype(F32))).astype(BF16))
    straight = jnp.concatenate(straight, axis=1)
    crossed = jnp.concatenate(crossed, axis=1)
    full = wall[...].reshape(n_col * 2 * M, YN)
    update[0, 0] = dot(straight, full, NN) * up_scale
    update[0, 1] = dot(crossed, full, NN) * up_scale

    for c in col_order[:-1]:
        col_copy(0, strip_out, strip_in, c, c, c).wait_send()
        col_copy(1, delta_out, delta_in, c, c, c).wait_send()
    for f in facet_order[:-1]:
        facet_copy(0, contrib_out, contrib_in, f, f, f).wait_send()
        facet_copy(1, back_out, back_in, f, f, f).wait_send()


def body(n_facet, n_col, facets, col_offsets, sub_rows, facet_offsets, vis_pos, observed):
    assert sub_rows.shape[0] == n_facet
    n_rows = facets.shape[2]
    n_vis = vis_pos.shape[3]
    vmem = pl.BlockSpec(memory_space=pltpu.VMEM)
    smem = pl.BlockSpec(memory_space=pltpu.SMEM)
    facet_blocks = pltpu.VMEM((n_facet, M, 2 * M), BF16)
    col_blocks = pltpu.VMEM((n_col, n_rows, 2 * M), BF16)
    table_rows = n_col + n_facet
    return tuple(
        pl.pallas_call(
            functools.partial(kernel, n_facet, n_col),
            out_shape=(
                jax.ShapeDtypeStruct(observed.shape, F32),
                jax.ShapeDtypeStruct(facets.shape, F32),
            ),
            in_specs=[pl.BlockSpec(memory_space=pl.ANY), smem, smem, smem, vmem, vmem],
            out_specs=(vmem, vmem),
            scratch_shapes=[
                pltpu.VMEM((2, n_rows, YN), BF16),
                pltpu.VMEM((2, M, YN), F32),
                pltpu.VMEM((2, table_rows, YN), F32),
                pltpu.VMEM((n_col, 2 * M, YN), BF16),
                pltpu.VMEM((n_facet, 2 * M, YN), BF16),
                pltpu.VMEM((YN, n_facet * 2 * M), BF16),
                pltpu.VMEM((n_facet, 2 * M, n_vis), BF16),
                pltpu.VMEM((n_facet, 2 * M, n_vis), F32),
                col_blocks,
                col_blocks,
                facet_blocks,
                facet_blocks,
                facet_blocks,
                facet_blocks,
                col_blocks,
                col_blocks,
                pltpu.SemaphoreType.DMA,
                pltpu.SemaphoreType.DMA((2, n_col)),
                pltpu.SemaphoreType.DMA((2, n_col)),
                pltpu.SemaphoreType.DMA((2, n_facet)),
                pltpu.SemaphoreType.DMA((2, n_facet)),
            ],
            compiler_params=pltpu.CompilerParams(collective_id=0, has_side_effects=True),
            name="predict_update",
        )(facets, col_offsets, sub_rows, facet_offsets, vis_pos, observed)
    )


def solution(mesh):
    in_specs = (
        P("facet", None, "col", None),
        P(),
        P(None, "col"),
        P(),
        P("facet", "col", None, None),
        P("facet", "col", None, None),
    )
    out_specs = (P("facet", "col", None, None), P("facet", None, "col", None))
    step = functools.partial(body, mesh.shape["facet"], mesh.shape["col"])
    return jax.shard_map(step, mesh=mesh, in_specs=in_specs, out_specs=out_specs, check_vma=False)
```

profile of v0, /device:TPU:0, one launch (start us, length us, event | category | flops | bytes accessed | tf_op | source)
XLA Modules:
  0.0 33.9 jit_solution(7551182311834512983)
XLA Ops:
  0.6 0.0 copy-start.1
  0.6 1.3 %copy.8.sub_rows = s32[4,1]{1,0:T(4,128)} copy(s32[4,1]{0,1:T(1,128)} %param.8) | data formatting | bytes 32 | tf_op args[2]
  2.0 0.0 copy-done.1
  2.0 0.7 %copy.9.facet_offsets = s32[4,2]{1,0:T(4,128)} copy(s32[4,2]{0,1:T(2,128)S(1)} %copy-done.1) | data formatting | bytes 64 | tf_op args[3]
  2.6 28.1 %predict_update.1 = (f32[1,1,2,256]{3,2,1,0:T(2,128)}, f32[1,2,96,768]{3,2,1,0:T(8,128)}) custom-call(bf16[1,2,96,768]{3,2,1,0:T(8,128)(2,1)} %facets_hbm.1, s32[8]{0:T(128)} %col_offsets.1, s32[4,1]{1,0:T(4,128)} %copy.8.sub_rows, s32[4,2]{1,0:T(4,128)} %copy.9.facet_offsets, s32[1,1,2,256]{3,2,1,0:T(2,128)} %vis_pos.1, f32[1,1,2,256]{3,2,1,0:T(2,128)} %observed.1), custom_call_target="tpu_custom_call" | custom-call | tf_op jit(solution)/shard_map/predict_update/pallas_call | solution.py:260
  30.7 0.0 copy-start
  30.7 0.7 %copy-done = f32[1,1,2,256]{3,2,1,0:T(2,128)S(1)} copy-done((f32[1,1,2,256]{3,2,1,0:T(2,128)S(1)}, f32[1,1,2,256]{3,2,1,0:T(2,128)}, u32[]{:S(2)}) %copy-start) | copy-done | bytes 2072
  31.4 0.6 %copy.12 = f32[1,1,2,256]{3,2,1,0:T(2,128)} copy(f32[1,1,2,256]{3,2,1,0:T(2,128)S(1)} %copy-done) | data formatting | bytes 4096
  31.9 1.9 %copy.13 = f32[1,2,96,768]{3,2,1,0:T(8,128)} copy(f32[1,2,96,768]{3,2,1,0:T(8,128)} %get-tuple-element.5) | data formatting | bytes 1179648
Async XLA Ops:
  0.6 1.3 %copy-start.1 = (s32[4,2]{0,1:T(2,128)S(1)}, s32[4,2]{0,1:T(2,128)}, u32[]{:S(2)}) copy-start(s32[4,2]{0,1:T(2,128)} %param.9) | copy-start | bytes 100
  30.7 0.7 %copy-start = (f32[1,1,2,256]{3,2,1,0:T(2,128)S(1)}, f32[1,1,2,256]{3,2,1,0:T(2,128)}, u32[]{:S(2)}) copy-start(f32[1,1,2,256]{3,2,1,0:T(2,128)} %get-tuple-element.4) | copy-start | bytes 6148
where the time goes:
time: 34.1 us; the launch traced here: 33.9 us
  Pallas kernels  28.1 us (82%)
  local copies, waits for them, and re-layouts  5.15 us (15%)
  between operations  0.66 us (2%)
    pallas_call x1, Pallas kernels, body(): pl.pallas_call(functools.partial(kernel, n_facet, n_col), out_shape=(jax....  28.1 us
    unnamed x8, local copies, waits for them, and re-layouts  5.15 us

commit v1 on v0

--- a/solution.py
+++ b/solution.py
@@ -12,6 +12,7 @@
 SUB = 384
 FINE = 1536
 YN = 768
+MARGIN = 8192
 MESH = pl.DeviceIdType.MESH
 F32 = jnp.float32
 BF16 = jnp.bfloat16
@@ -43,14 +44,19 @@
     n_facet,
     n_col,
     facets_hbm,
+    col_offsets_hbm,
+    sub_rows_hbm,
+    facet_offsets_hbm,
+    vis_pos_hbm,
+    observed_hbm,
+    predicted,
+    update,
+    facet_buf,
     col_offsets,
     sub_rows,
     facet_offsets,
     vis_pos,
     observed,
-    predicted,
-    update,
-    facet_buf,
     base,
     turn,
     wall,
@@ -77,11 +83,29 @@
     n_rows = facet_buf.shape[1]
     n_vis = vis_pos.shape[3]
 
-    load = pltpu.make_async_copy(facets_hbm.at[0], facet_buf, load_sem)
-    load.start()
+    loads = [
+        pltpu.make_async_copy(source, held, load_sem.at[i])
+        for i, (source, held) in enumerate(
+            (
+                (col_offsets_hbm, col_offsets),
+                (sub_rows_hbm, sub_rows),
+                (facets_hbm.at[0], facet_buf),
+                (facet_offsets_hbm, facet_offsets),
+                (vis_pos_hbm, vis_pos),
+                (observed_hbm, observed),
+            )
+        )
+    ]
+    for load in loads:
+        load.start()
     barrier = pltpu.get_barrier_semaphore()
-    col_order = [lax.rem(my_c + n_col // 2 + i, n_col) for i in range(n_col)]
-    col_order = [c for i, c in enumerate(col_order) if i != n_col // 2] + [my_c]
+    n_pair = n_col // 2
+    my_pair, my_core = my_c // 2, lax.rem(my_c, 2)
+    steps = sorted(range(1, n_pair), key=lambda step: -min(step, n_pair - step)) + [0]
+    pair_order = [lax.rem(my_pair + step, n_pair) for step in steps]
+    col_order = []
+    for pair in pair_order:
+        col_order += [2 * pair + 1 - my_core, 2 * pair + my_core]
     facet_order = [lax.rem(my_f + 1 + i, n_facet) for i in range(n_facet)]
     for c in col_order[:-1]:
         pl.semaphore_signal(barrier, inc=1, device_id=(my_f, c), device_id_type=MESH)
@@ -113,10 +137,12 @@
     base[0] = base_re * inv_root
     base[1] = base_im * inv_root
     along = iota((1, YN), 1)
+    loads[0].wait()
+    loads[1].wait()
     for c in range(n_col):
         turn[0, pl.ds(c, 1)] = along * col_offsets[c].astype(F32)
     for s in range(n_facet):
-        turn[0, pl.ds(n_col + s, 1)] = along * sub_rows[s, 0].astype(F32)
+        turn[0, pl.ds(n_col + s, 1)] = along * sub_rows[0, s].astype(F32)
     turn_re, turn_im = cis(turn[0], YN, -1.0)
     turn[0] = turn_re
     turn[1] = turn_im
@@ -132,33 +158,39 @@
     def swapped(value):
         return pltpu.roll(value, M, 1)
 
-    load.wait()
+    loads[2].wait()
     both = facet_buf[...]
     if n_rows % 16:
         both = both.astype(F32).reshape(2 * n_rows, YN).astype(BF16)
     else:
         both = both.reshape(2 * n_rows, YN)
+    early = n_col // 2
     for i, c in enumerate(col_order):
         table(wall, c, c)
         prod = dot(both, wall[c], NT)
         part = (prod[:n_rows] + minus_plus * swapped(prod[n_rows:])).astype(BF16)
-        if i == 0:
-            pl.semaphore_wait(barrier, n_col - 1 + n_facet - 1)
         if i < n_col - 1:
             strip_out[c] = part
-            col_copy(0, strip_out, strip_in, c, my_c, c).start()
         else:
             strip_in[c] = part
+        if i == early - 1:
+            pl.semaphore_wait(barrier, n_col - 1 + n_facet - 1)
+            for ready in col_order[:early]:
+                col_copy(0, strip_out, strip_in, ready, my_c, ready).start()
+        elif early <= i < n_col - 1:
+            col_copy(0, strip_out, strip_in, c, my_c, c).start()
 
     for s in range(n_facet):
         table(subt, n_col + s, s)
+    for load in loads[3:]:
+        load.wait()
     for tab, which in ((u_tab, 0), (v_tab, 1)):
         point = vis_pos[0, 0, pl.ds(which, 1)].astype(F32)
         low_re, low_im = cis(iota((M, n_vis), 0) * point, FINE, 1.0)
         low_re = low_re * (1.0 / math.sqrt(SUB))
         low_im = low_im * (1.0 / math.sqrt(SUB))
         for f in range(n_facet):
-            high_re, high_im = cis(point * facet_offsets[f, which].astype(F32), FINE, 1.0)
+            high_re, high_im = cis(point * facet_offsets[which, f].astype(F32), FINE, 1.0)
             tab[f, :M] = (low_re * high_re - low_im * high_im).astype(tab.dtype)
             tab[f, M:] = (low_re * high_im + low_im * high_re).astype(tab.dtype)
     for s in range(n_facet):
@@ -171,14 +203,14 @@
         strip = strip.astype(F32).reshape(YN, 2 * M).astype(BF16)
     else:
         strip = strip.reshape(YN, 2 * M)
-    for i, s in enumerate(facet_order):
-        prod = dot(subt[s], strip, NN)
-        part = (prod[:M] + minus_plus * swapped(prod[M:])).astype(BF16)
-        if i < n_facet - 1:
-            contrib_out[s] = part
-            facet_copy(0, contrib_out, contrib_in, s, my_f, s).start()
-        else:
-            contrib_in[s] = part
+    prod = dot(subt[...].reshape(n_facet * 2 * M, YN), strip, NN)
+    for s in range(n_facet):
+        top = prod[2 * M * s : 2 * M * s + M]
+        low = prod[2 * M * s + M : 2 * M * (s + 1)]
+        contrib_out[s] = (top + minus_plus * swapped(low)).astype(BF16)
+    for s in facet_order[:-1]:
+        facet_copy(0, contrib_out, contrib_in, s, my_f, s).start()
+    contrib_in[my_f] = contrib_out[my_f]
 
     pred_re = jnp.zeros((M, n_vis), F32)
     pred_im = jnp.zeros((M, n_vis), F32)
@@ -219,25 +251,30 @@
         block = back_in[s]
         stacked += [block, (-minus_plus * swapped(block.astype(F32))).astype(BF16)]
     back_scale = math.sqrt(YN / (M * n_facet))
-    delta = dot(subt_t[...], jnp.concatenate(stacked, axis=0), NN) * back_scale
-    delta_out[...] = delta.reshape(n_col, n_rows, 2 * M).astype(BF16)
-    for c in col_order[:-1]:
-        col_copy(1, delta_out, delta_in, c, my_c, c).start()
+    stacked = jnp.concatenate(stacked, axis=0)
+    for i, pair in enumerate(pair_order):
+        start = pl.multiple_of(pair * (2 * n_rows), 2 * n_rows)
+        delta = dot(subt_t[pl.ds(start, 2 * n_rows)], stacked, NN) * back_scale
+        delta_out[pl.ds(2 * pair, 2)] = delta.reshape(2, n_rows, 2 * M).astype(BF16)
+        for c in col_order[2 * i : 2 * i + 2]:
+            if c is not col_order[-1]:
+                col_copy(1, delta_out, delta_in, c, my_c, c).start()
     delta_in[my_c] = delta_out[my_c]
 
-    for c in col_order[:-1]:
-        col_copy(1, delta_out, delta_in, c, c, c).wait_recv()
     up_scale = math.sqrt(YN / (M * n_col))
-    straight, crossed = [], []
-    for c in range(n_col):
-        block = delta_in[c]
-        straight.append(block)
-        crossed.append((-minus_plus * swapped(block.astype(F32))).astype(BF16))
-    straight = jnp.concatenate(straight, axis=1)
-    crossed = jnp.concatenate(crossed, axis=1)
-    full = wall[...].reshape(n_col * 2 * M, YN)
-    update[0, 0] = dot(straight, full, NN) * up_scale
-    update[0, 1] = dot(crossed, full, NN) * up_scale
+    for i in reversed(range(n_pair)):
+        for c in col_order[2 * i : 2 * i + 2]:
+            if c is not col_order[-1]:
+                col_copy(1, delta_out, delta_in, c, c, c).wait_recv()
+        pair = pair_order[i]
+        blocks = [delta_in[2 * pair + core] for core in range(2)]
+        turned = [(-minus_plus * swapped(block.astype(F32))).astype(BF16) for block in blocks]
+        walls = wall[pl.ds(2 * pair, 2)].reshape(4 * M, YN)
+        for part, sides in enumerate((blocks, turned)):
+            term = dot(jnp.concatenate(sides, axis=1), walls, NN)
+            if i < n_pair - 1:
+                term += update[0, part]
+            update[0, part] = term * up_scale if i == 0 else term
 
     for c in col_order[:-1]:
         col_copy(0, strip_out, strip_in, c, c, c).wait_send()
@@ -247,26 +284,55 @@
         facet_copy(1, back_out, back_in, f, f, f).wait_send()
 
 
+def deliver_kernel(predicted, update, predicted_hbm, update_hbm, sems):
+    copies = [
+        pltpu.make_async_copy(update, update_hbm, sems.at[0]),
+        pltpu.make_async_copy(predicted, predicted_hbm, sems.at[1]),
+    ]
+    for copy in copies:
+        copy.start()
+    for copy in copies:
+        copy.wait()
+
+
+def deliver(predicted, update):
+    vmem = pl.BlockSpec(memory_space=pltpu.VMEM)
+    hbm = pl.BlockSpec(memory_space=pltpu.HBM)
+    return pl.pallas_call(
+        deliver_kernel,
+        out_shape=(
+            jax.ShapeDtypeStruct(predicted.shape, F32),
+            jax.ShapeDtypeStruct(update.shape, F32),
+        ),
+        in_specs=[vmem, vmem],
+        out_specs=(hbm, hbm),
+        scratch_shapes=[pltpu.SemaphoreType.DMA((2,))],
+        compiler_params=pltpu.CompilerParams(vmem_limit_bytes=2**20),
+        name="deliver",
+    )(predicted, update)
+
+
 def body(n_facet, n_col, facets, col_offsets, sub_rows, facet_offsets, vis_pos, observed):
     assert sub_rows.shape[0] == n_facet
     n_rows = facets.shape[2]
     n_vis = vis_pos.shape[3]
     vmem = pl.BlockSpec(memory_space=pltpu.VMEM)
-    smem = pl.BlockSpec(memory_space=pltpu.SMEM)
     facet_blocks = pltpu.VMEM((n_facet, M, 2 * M), BF16)
     col_blocks = pltpu.VMEM((n_col, n_rows, 2 * M), BF16)
     table_rows = n_col + n_facet
-    return tuple(
-        pl.pallas_call(
+    vmem_left = (67043328 - 4 * (facets.size + observed.size)) // 1024 * 1024 - MARGIN
+    results = pl.pallas_call(
             functools.partial(kernel, n_facet, n_col),
-            out_shape=(
-                jax.ShapeDtypeStruct(observed.shape, F32),
-                jax.ShapeDtypeStruct(facets.shape, F32),
-            ),
-            in_specs=[pl.BlockSpec(memory_space=pl.ANY), smem, smem, smem, vmem, vmem],
+            out_shape=(pltpu.VMEM(observed.shape, F32), pltpu.VMEM(facets.shape, F32)),
+            in_specs=[pl.BlockSpec(memory_space=pltpu.HBM)] * 6,
             out_specs=(vmem, vmem),
             scratch_shapes=[
                 pltpu.VMEM((2, n_rows, YN), BF16),
+                pltpu.SMEM(col_offsets.shape, jnp.int32),
+                pltpu.SMEM(sub_rows.shape[::-1], jnp.int32),
+                pltpu.SMEM(facet_offsets.shape[::-1], jnp.int32),
+                pltpu.VMEM(vis_pos.shape, jnp.int32),
+                pltpu.VMEM(observed.shape, F32),
                 pltpu.VMEM((2, M, YN), F32),
                 pltpu.VMEM((2, table_rows, YN), F32),
                 pltpu.VMEM((n_col, 2 * M, YN), BF16),
@@ -282,16 +348,18 @@
                 facet_blocks,
                 col_blocks,
                 col_blocks,
-                pltpu.SemaphoreType.DMA,
+                pltpu.SemaphoreType.DMA((6,)),
                 pltpu.SemaphoreType.DMA((2, n_col)),
                 pltpu.SemaphoreType.DMA((2, n_col)),
                 pltpu.SemaphoreType.DMA((2, n_facet)),
                 pltpu.SemaphoreType.DMA((2, n_facet)),
             ],
-            compiler_params=pltpu.CompilerParams(collective_id=0, has_side_effects=True),
+            compiler_params=pltpu.CompilerParams(
+                collective_id=0, has_side_effects=True, vmem_limit_bytes=vmem_left
+            ),
             name="predict_update",
-        )(facets, col_offsets, sub_rows, facet_offsets, vis_pos, observed)
-    )
+        )(facets, col_offsets, sub_rows.T, facet_offsets.T, vis_pos, observed)
+    return deliver(*results)
 
 
 def solution(mesh):

time: 34.1 us -> 27.1 us (0.79)
  local copies, waits for them, and re-layouts: 5.15 us -> 0 us
  Pallas kernels: 28.1 us -> 26.3 us
    unnamed x8 -> x0, local copies, waits for them, and re-layouts: 5.15 us -> none
    pallas_call x1 -> x2, Pallas kernels: 28.1 us -> 26.3 us  [the longest x1 25.5 us: body(): pl.pallas_call(functools.partial(kernel, n_facet, n_col), out_shape=(pltp...]
where the time goes in v1:
time: 27.1 us; the launch traced here: 27 us
  Pallas kernels  26.3 us (97%)
  between operations  0.64 us (2%)
    pallas_call x1, Pallas kernels, body(): pl.pallas_call(functools.partial(kernel, n_facet, n_col), out_shape=(pltp...  25.5 us
    pallas_call x1, Pallas kernels, deliver(): pl.pallas_call(deliver_kernel, out_shape=(jax.ShapeDtypeStruct(predicted....  0.84 us

profile of v1, /device:TPU:0, one launch (start us, length us, event | category | flops | bytes accessed | tf_op | source)
XLA Modules:
  0.0 27.0 jit_solution(15588275670001844871)
XLA Ops:
  0.6 25.5 %predict_update.1 = (f32[1,1,2,256]{3,2,1,0:T(2,128)S(1)}, f32[1,2,96,768]{3,2,1,0:T(8,128)S(1)}) custom-call(bf16[1,2,96,768]{3,2,1,0:T(8,128)(2,1)} %facets_hbm.1, s32[8]{0:T(128)} %col_offsets_hbm.1, s32[1,4]{1,0:T(1,128)} %bitcast.3, s32[2,4]{1,0:T(2,128)} %bitcast.2, s32[1,1,2,256]{3,2,1,0:T(2,128)} %vis_pos_hbm.1, f32[1,1,2,256]{3,2,1,0:T(2,128)} %observed_hbm.1), custom_call_target="tpu_custom_call" | custom-call | tf_op jit(solution)/shard_map/predict_update/pallas_call | solution.py:324
  26.1 0.8 %deliver.1 = (f32[1,1,2,256]{3,2,1,0:T(2,128)}, f32[1,2,96,768]{3,2,1,0:T(8,128)}) custom-call(f32[1,1,2,256]{3,2,1,0:T(2,128)S(1)} %get-tuple-element.4.predicted, f32[1,2,96,768]{3,2,1,0:T(8,128)S(1)} %get-tuple-element.5.update), custom_call_target="tpu_custom_call" | custom-call | tf_op jit(solution)/shard_map/deliver/pallas_call | solution.py:301

commit v2 on v1

--- a/solution.py
+++ b/solution.py
@@ -101,8 +101,13 @@
     barrier = pltpu.get_barrier_semaphore()
     n_pair = n_col // 2
     my_pair, my_core = my_c // 2, lax.rem(my_c, 2)
-    steps = sorted(range(1, n_pair), key=lambda step: -min(step, n_pair - step)) + [0]
-    pair_order = [lax.rem(my_pair + step, n_pair) for step in steps]
+    side = my_pair // (n_pair // 2)
+    mirrored = my_pair + side * (n_pair - 1 - 2 * my_pair)
+    pair_order = []
+    for place in range(n_pair - 1, 0, -1):
+        target = place - (mirrored + n_pair - place) // n_pair
+        pair_order.append(target + side * (n_pair - 1 - 2 * target))
+    pair_order.append(my_pair)
     col_order = []
     for pair in pair_order:
         col_order += [2 * pair + 1 - my_core, 2 * pair + my_core]
@@ -164,7 +169,7 @@
         both = both.astype(F32).reshape(2 * n_rows, YN).astype(BF16)
     else:
         both = both.reshape(2 * n_rows, YN)
-    early = n_col // 2
+    early = n_col - 1
     for i, c in enumerate(col_order):
         table(wall, c, c)
         prod = dot(both, wall[c], NT)

time: 27.1 us -> 26.7 us (0.985)
  Pallas kernels: 26.3 us -> 25.9 us
    pallas_call x1, Pallas kernels: 25.5 us -> 25.1 us  [body(): pl.pallas_call(functools.partial(kernel, n_facet, n_col), out_shape=(pltp...]
where the time goes in v2:
time: 26.7 us; the launch traced here: 26.6 us
  Pallas kernels  25.9 us (97%)
  between operations  0.64 us (2%)
    pallas_call x1, Pallas kernels, body(): pl.pallas_call(functools.partial(kernel, n_facet, n_col), out_shape=(pltp...  25.1 us
    pallas_call x1, Pallas kernels, deliver(): pl.pallas_call(deliver_kernel, out_shape=(jax.ShapeDtypeStruct(predicted....  0.84 us

profile of v2, /device:TPU:0, one launch (start us, length us, event | category | flops | bytes accessed | tf_op | source)
XLA Modules:
  0.0 26.6 jit_solution(6604304441745338120)
XLA Ops:
  0.6 25.1 %predict_update.1 = (f32[1,1,2,256]{3,2,1,0:T(2,128)S(1)}, f32[1,2,96,768]{3,2,1,0:T(8,128)S(1)}) custom-call(bf16[1,2,96,768]{3,2,1,0:T(8,128)(2,1)} %facets_hbm.1, s32[8]{0:T(128)} %col_offsets_hbm.1, s32[1,4]{1,0:T(1,128)} %bitcast.3, s32[2,4]{1,0:T(2,128)} %bitcast.2, s32[1,1,2,256]{3,2,1,0:T(2,128)} %vis_pos_hbm.1, f32[1,1,2,256]{3,2,1,0:T(2,128)} %observed_hbm.1), custom_call_target="tpu_custom_call" | custom-call | tf_op jit(solution)/shard_map/predict_update/pallas_call | solution.py:329
  25.7 0.8 %deliver.1 = (f32[1,1,2,256]{3,2,1,0:T(2,128)}, f32[1,2,96,768]{3,2,1,0:T(8,128)}) custom-call(f32[1,1,2,256]{3,2,1,0:T(2,128)S(1)} %get-tuple-element.4.predicted, f32[1,2,96,768]{3,2,1,0:T(8,128)S(1)} %get-tuple-element.5.update), custom_call_target="tpu_custom_call" | custom-call | tf_op jit(solution)/shard_map/deliver/pallas_call | solution.py:306

commit v3 on v2

--- a/solution.py
+++ b/solution.py
@@ -208,14 +208,14 @@
         strip = strip.astype(F32).reshape(YN, 2 * M).astype(BF16)
     else:
         strip = strip.reshape(YN, 2 * M)
-    prod = dot(subt[...].reshape(n_facet * 2 * M, YN), strip, NN)
-    for s in range(n_facet):
-        top = prod[2 * M * s : 2 * M * s + M]
-        low = prod[2 * M * s + M : 2 * M * (s + 1)]
-        contrib_out[s] = (top + minus_plus * swapped(low)).astype(BF16)
-    for s in facet_order[:-1]:
-        facet_copy(0, contrib_out, contrib_in, s, my_f, s).start()
-    contrib_in[my_f] = contrib_out[my_f]
+    for i, s in enumerate(facet_order):
+        prod = dot(subt[s], strip, NN)
+        part = (prod[:M] + minus_plus * swapped(prod[M:])).astype(BF16)
+        if i < n_facet - 1:
+            contrib_out[s] = part
+            facet_copy(0, contrib_out, contrib_in, s, my_f, s).start()
+        else:
+            contrib_in[s] = part
 
     pred_re = jnp.zeros((M, n_vis), F32)
     pred_im = jnp.zeros((M, n_vis), F32)

time: 26.7 us -> 26.6 us (level)
  no operation moved by 1% of the time
where the time goes in v3:
time: 26.6 us; the launch traced here: 26.5 us
  Pallas kernels  25.9 us (97%)
  between operations  0.64 us (2%)
    pallas_call x1, Pallas kernels, body(): pl.pallas_call(functools.partial(kernel, n_facet, n_col), out_shape=(pltp...  25 us
    pallas_call x1, Pallas kernels, deliver(): pl.pallas_call(deliver_kernel, out_shape=(jax.ShapeDtypeStruct(predicted....  0.84 us

profile of v3, /device:TPU:0, one launch (start us, length us, event | category | flops | bytes accessed | tf_op | source)
XLA Modules:
  0.0 26.5 jit_solution(4082715772705402983)
XLA Ops:
  0.6 25.0 %predict_update.1 = (f32[1,1,2,256]{3,2,1,0:T(2,128)S(1)}, f32[1,2,96,768]{3,2,1,0:T(8,128)S(1)}) custom-call(bf16[1,2,96,768]{3,2,1,0:T(8,128)(2,1)} %facets_hbm.1, s32[8]{0:T(128)} %col_offsets_hbm.1, s32[1,4]{1,0:T(1,128)} %bitcast.3, s32[2,4]{1,0:T(2,128)} %bitcast.2, s32[1,1,2,256]{3,2,1,0:T(2,128)} %vis_pos_hbm.1, f32[1,1,2,256]{3,2,1,0:T(2,128)} %observed_hbm.1), custom_call_target="tpu_custom_call" | custom-call | tf_op jit(solution)/shard_map/predict_update/pallas_call | solution.py:329
  25.7 0.8 %deliver.1 = (f32[1,1,2,256]{3,2,1,0:T(2,128)}, f32[1,2,96,768]{3,2,1,0:T(8,128)}) custom-call(f32[1,1,2,256]{3,2,1,0:T(2,128)S(1)} %get-tuple-element.4.predicted, f32[1,2,96,768]{3,2,1,0:T(8,128)S(1)} %get-tuple-element.5.update), custom_call_target="tpu_custom_call" | custom-call | tf_op jit(solution)/shard_map/deliver/pallas_call | solution.py:306
